TPU v7x, 8 devices: a whole 2x2x1 slice. The times are simulated.
8 devices in a mesh: dp: 2 (over y, z), tp: 4 (over x, core).
Axes of the slice: x: 2, y: 2, z: 1, core: 2. Of those that a mesh axis runs over, the one named last changes fastest.
Arguments:
- x: bfloat16 [128, 4096], P('dp'), parts along dimension 0
- k_cache: bfloat16 [128, 2048, 8, 128], P('dp', None, 'tp'), parts along dimension 0
- v_cache: bfloat16 [128, 2048, 8, 128], P('dp', None, 'tp'), parts along dimension 0
- gain_a: bfloat16 [4096], replicated
- wq: bfloat16 [4096, 4096], P(None, 'tp')
- wo: bfloat16 [4096, 4096], P('tp')
- gain_m: bfloat16 [4096], replicated
- w_gate: bfloat16 [4096, 14336], P(None, 'tp')
- w_up: bfloat16 [4096, 14336], P(None, 'tp')
- w_down: bfloat16 [14336, 4096], P('tp')
Outputs:
- output: bfloat16 [128, 4096], P('dp'), parts along dimension 0
There are 2 independent parts. A program takes and returns all parts, laid end to end along the dimension named above; an argument that names none is the same for every part.
All inputs are finite; a program needn't handle non-finite values.
Results may differ from a plain program's by a relative error of at most 0.017.
Values are sent between devices in bfloat16 or wider.
A program may use at most 2 GiB of HBM per device.

v0:
```python
import jax
import jax.numpy as jnp
from jax import lax
from jax.sharding import PartitionSpec as P

HEAD = 128
THETA = 10000


def normed(x, gain):
    wide = x.astype(jnp.float32)
    scale = lax.rsqrt(jnp.mean(wide * wide, -1, keepdims=True) + 1e-6)
    return (wide * scale * gain.astype(jnp.float32)).astype(jnp.bfloat16)


def turned(t, place, theta):
    half = t.shape[-1] // 2
    angle = place.astype(jnp.float32)[:, None] * theta ** (-jnp.arange(half, dtype=jnp.float32) / half)
    cos, sin = jnp.cos(angle)[:, None], jnp.sin(angle)[:, None]
    a, b = t[..., :half].astype(jnp.float32), t[..., half:].astype(jnp.float32)
    return jnp.concatenate([a * cos - b * sin, b * cos + a * sin], -1).astype(jnp.bfloat16)


def matmul(a, w):
    return jnp.dot(a, w, preferred_element_type=jnp.float32).astype(jnp.bfloat16)


def einsum(form, a, b):
    return jnp.einsum(form, a.astype(jnp.float32), b.astype(jnp.float32))


def seen_by(a, wq, k_cache, v_cache, head, theta):
    batch, cache, kv_heads = k_cache.shape[:3]
    place = jnp.full((batch,), cache - 1)
    q = turned(matmul(a, wq).reshape(batch, -1, head), place, theta).reshape(batch, kv_heads, -1, head)
    scores = einsum("bgsd,bugd->bgsu", q, k_cache) * head**-0.5
    weights = jax.nn.softmax(scores, -1).astype(jnp.bfloat16)
    return einsum("bgsu,bugd->bgsd", weights, v_cache).astype(jnp.bfloat16).reshape(batch, -1)


def hidden_of(b, w_gate, w_up):
    gate = jnp.dot(b, w_gate, preferred_element_type=jnp.float32)
    up = jnp.dot(b, w_up, preferred_element_type=jnp.float32)
    return (jax.nn.silu(gate) * up).astype(jnp.bfloat16)


def solution(mesh):
    def added(t, term):
        return (t.astype(jnp.float32) + lax.psum(term.astype(jnp.bfloat16), "tp").astype(jnp.float32)).astype(jnp.bfloat16)

    def step(x, k_cache, v_cache, gain_a, wq, wo, gain_m, w_gate, w_up, w_down):
        seen = seen_by(normed(x, gain_a), wq, k_cache, v_cache, HEAD, THETA)
        h = added(x, jnp.dot(seen, wo, preferred_element_type=jnp.float32))
        return added(h, jnp.dot(hidden_of(normed(h, gain_m), w_gate, w_up), w_down, preferred_element_type=jnp.float32))

    states, cache, columns, rows_of = P("dp", None), P("dp", None, "tp", None), P(None, "tp"), P("tp", None)
    return jax.shard_map(
        step,
        mesh=mesh,
        in_specs=(states, cache, cache, P(None), columns, rows_of, P(None), columns, columns, rows_of),
        out_specs=states,
        check_vma=False,
    )
```

profile of v0, /device:TPU:0, one launch (start us, length us, event | category | flops | bytes accessed | tf_op | source)
XLA Modules:
  0.0 185.6 jit_solution(14986008335950889581)
XLA Ops:
  6.5 0.0 all-reduce.3.cloned.1.call-start
  6.6 0.7 convert_element_type.63
  7.3 1.2 fusion.13
  8.6 5.2 %fusion.12 = bf16[8,8,8,128]{3,1,2,0:T(8,128)(2,1)S(1)} fusion(bf16[4096,1024]{1,0:T(8,128)(2,1)} %param.14, bf16[64,4096]{1,0:T(8,128)(2,1)} %param.10, f32[4096]{0:T(1024)S(1)} %convert_element_type.63, f32[64]{0:T(128)S(1)} %add_rsqrt_fusion.1), kind=kOutput, calls=%fused_computation.23 | convolution fusion | flops 537985024 | bytes 9060608 | tf_op jit(solution)/shard_map/dot_general | solution.py:25
  13.8 0.1 fusion.31
  13.9 35.4 %fusion.47 = (f32[64,2,4]{2,1,0:T(2,128)S(1)}, f32[64,2,4,2048]{3,2,1,0:T(4,128)}) fusion(bf16[64,2048,2,128]{3,2,1,0:T(2,128)(2,1)} %param.11, bf16[64,2,4,64]{3,2,1,0:T(4,128)(2,1)S(1)} %bitcast.13, bf16[64,2,4,64]{3,2,1,0:T(4,128)(2,1)S(1)} %bitcast.12), kind=kOutput, calls=%fused_computation.60 | convolution fusion | flops 271845376 | bytes 71436288 | tf_op jit(solution)/shard_map/sub | solution.py:37
  49.4 0.0 copy-start.1
  49.4 0.0 copy-start
  49.4 26.6 %fusion.9 = bf16[64,2,4,128]{3,2,1,0:T(4,128)(2,1)S(1)} fusion(bf16[64,2048,2,128]{3,2,1,0:T(2,128)(2,1)} %param.12, f32[64,2,4,2048]{3,2,1,0:T(4,128)} %get-tuple-element.10, f32[64,2,4]{2,1,0:T(2,128)S(1)} %get-tuple-element.9), kind=kOutput, calls=%fused_computation.22 | convolution fusion | flops 270598144 | bytes 71436288 | tf_op jit(solution)/shard_map/bgsu,bugd->bgsd/dot_general | solution.py:29
  76.0 0.1 reshape.40
  76.0 5.7 %convolution_convert_fusion = bf16[64,4096]{1,0:T(8,128)(2,1)} fusion(bf16[64,1024]{1,0:T(8,128)(2,1)S(1)} %reshape.40, bf16[1024,4096]{1,0:T(8,128)(2,1)} %param.15), kind=kOutput, calls=%fused_computation.6 | convolution fusion | flops 537133056 | bytes 9043968 | tf_op jit(solution)/shard_map/dot_general | solution.py:53
  81.8 0.0 all-reduce.3.cloned.1.call-update
  81.8 0.2 all-reduce.5.cloned.1.call-start
  82.0 0.0 copy-done.1
  82.1 30.5 %all-reduce.3.cloned.1.call-done = bf16[64,4096]{1,0:T(8,128)(2,1)} async-done(((bf16[64,4096]{1,0:T(8,128)(2,1)}), bf16[64,4096]{1,0:T(8,128)(2,1)}) %all-reduce.3.cloned.1.call-update) | async-done | bytes 524304 | tf_op jit(solution)/shard_map/psum | solution.py:49
  112.6 0.0 copy-done
  112.6 1.3 fusion.17
  113.9 12.1 %fusion.36 = f32[64,3584]{1,0:T(8,128)S(1)} fusion(bf16[4096,3584]{1,0:T(8,128)(2,1)} %param.17, bf16[64,4096]{1,0:T(8,128)(2,1)S(1)} %get-tuple-element.6, f32[4096]{0:T(1024)S(1)} %convert_element_type.74, f32[64]{0:T(128)S(1)} %add_rsqrt_fusion), kind=kOutput, calls=%fused_computation.48 | convolution fusion | flops 1880096768 | bytes 30818560 | tf_op jit(solution)/shard_map/dot_general | solution.py:42
  126.0 22.9 %convolution_convert_fusion.1 = bf16[64,4096]{1,0:T(8,128)(2,1)} fusion(bf16[3584,4096]{1,0:T(8,128)(2,1)} %param.19, bf16[4096,3584]{1,0:T(8,128)(2,1)} %param.18, f32[64,3584]{1,0:T(8,128)S(1)} %fusion.36, bf16[64,4096]{1,0:T(8,128)(2,1)S(1)} %get-tuple-element.6, f32[4096]{0:T(1024)S(1)} %convert_element_type.74, f32[64]{0:T(128)S(1)} %add_rsqrt_fusion), kind=kOutput, calls=%fused_computation.8 | convolution fusion | flops 3760783360 | bytes 60702976 | tf_op jit(solution)/shard_map/dot_general | solution.py:54
  148.9 0.0 all-reduce.5.cloned.1.call-update
  148.9 27.9 %all-reduce.5.cloned.1.call-done = bf16[64,4096]{1,0:T(8,128)(2,1)} async-done(((bf16[64,4096]{1,0:T(8,128)(2,1)}), bf16[64,4096]{1,0:T(8,128)(2,1)}) %all-reduce.5.cloned.1.call-update) | async-done | bytes 524304 | tf_op jit(solution)/shard_map/psum | solution.py:49
  176.8 2.0 %fusion.20 = bf16[64,4096]{1,0:T(8,128)(2,1)} fusion(bf16[64,4096]{1,0:T(8,128)(2,1)S(1)} %get-tuple-element.6, bf16[64,4096]{1,0:T(8,128)(2,1)} %all-reduce.5.cloned.1.call-done), kind=kLoop, calls=%fused_computation.31 | loop fusion | flops 1048576 | bytes 1572864 | tf_op jit(solution)/shard_map/convert_element_type | solution.py:49
  (5 shorter events, 0.1 us)
Async XLA Ops:
  6.5 106.0 %all-reduce.3.cloned.1.call-start = ((), (), s32[]{:S(2)}) async-start(), calls=%async_computation | async-start | bytes 1048576 | tf_op jit(solution)/shard_map/psum | solution.py:49
  49.4 32.7 %copy-start.1 = (bf16[4096]{0:T(1024)(128)(2,1)S(1)}, bf16[4096]{0:T(1024)(128)(2,1)}, u32[]{:S(2)}) copy-start(bf16[4096]{0:T(1024)(128)(2,1)} %param.16) | copy-start | bytes 24580
  49.4 63.2 %copy-start = (bf16[64,4096]{1,0:T(8,128)(2,1)S(1)}, bf16[64,4096]{1,0:T(8,128)(2,1)}, u32[]{:S(2)}) copy-start(bf16[64,4096]{1,0:T(8,128)(2,1)} %param.10) | copy-start | bytes 1572868
  81.8 95.0 %all-reduce.5.cloned.1.call-start = ((), (), s32[]{:S(2)}) async-start(), calls=%async_computation.1 | async-start | bytes 1048576 | tf_op jit(solution)/shard_map/psum | solution.py:49
Sparse Core Ops, SparseCore 0:
  81.9 30.5 all-reduce.2
  149.0 27.7 all-reduce.4
where the time goes:
time: 186 us
  matrix products  108 us (58%)
  waiting for transfers between devices  58.4 us (31%)
  between operations  13.5 us (7%)
  other arithmetic  5.43 us (3%)
    psum x2, waiting for transfers between devices, added(): lax.psum(term.astype(jnp.bfloat16), 'tp').astype(jnp.float32)  58.4 us
    sub x1, matrix products, seen_by(): weights = jax.nn.softmax(scores, -1).astype(jnp.bfloat16)  35.4 us
    dot_general x1, matrix products, einsum(): return jnp.einsum(form, a.astype(jnp.float32), b.astype(jnp.float32))  26.6 us
    dot_general x1, matrix products, step(): jnp.dot(hidden_of(normed(h, gain_m), w_gate, w_up), w_down, preferred_ele...  22.9 us
    dot_general x1, matrix products, hidden_of(): gate = jnp.dot(b, w_gate, preferred_element_type=jnp.float32)  12.1 us
    dot_general x1, matrix products, step(): h = added(x, jnp.dot(seen, wo, preferred_element_type=jnp.float32))  5.75 us
    dot_general x1, matrix products, matmul(): jnp.dot(a, w, preferred_element_type=jnp.float32).astype(jnp.bfloat16)  5.2 us
  transfers between devices with their start and end apart: 2, of which 2 were waited for; matrix products, arithmetic and copies ran while one was open for 0% of the time, Pallas kernels for 0%

commit v1 on v0

v1 whole, which is shorter than its diff:
```python
import jax
import jax.numpy as jnp
import numpy as np
from jax import lax
from jax.experimental import pallas as pl
from jax.experimental.pallas import tpu as pltpu
from jax.sharding import PartitionSpec as P

HEAD = 128
THETA = 10000
BATCH = 64
CACHE = 2048
KV = 2
D = 4096
FF = 3584
ROWS, COLS = 1024, 512
SB = 4
R = 12
GROUPS = BATCH // SB
TILE = 256
NT = D // TILE
NB = D // COLS
NF = FF // COLS
Q_K0, Q_KV, Q_VL, Q_WO, Q_GU, Q_WD = 2, 3, 33, 34, 36, 50
F32, BF16 = jnp.float32, jnp.bfloat16
NEG = float("-inf")


def kernel(x_hbm, k_hbm, v_hbm, ga_hbm, wq, wo, gm_hbm, wg, wu, wd, rot_hbm, out,
           ring, xb, ab, gb, rb, qb, sca, scb, seen, hid, f1, s1, r1, s2, r2, y,
           sem, xsem, gsem, ss1, rs1, ss2, rs2, ss3, rs3, osem):
    tp = lax.axis_index("tp")
    k = lax.rem(tp, 2)
    sib = tp + 1 - 2 * k
    far = lax.rem(tp + 2, 4)

    def slot(quad, s):
        return (quad % R if isinstance(quad, int) else lax.rem(quad, R)) * SB + s

    def put(src, dst, s):
        pltpu.make_async_copy(src, dst, s).start()

    def issue_wq(nc):
        for s in range(SB):
            i = slot(nc, s)
            put(wq.at[pl.ds(s * ROWS, ROWS), pl.ds(nc * COLS, COLS)], ring.at[i], sem.at[i])

    def issue_kv(ref, g, quad):
        for s in range(SB):
            i = slot(quad, s)
            for c in range(4):
                put(ref.at[g * SB + s, pl.ds(c * ROWS, ROWS), :], ring.at[i, :, pl.ds(c * 128, 128)], sem.at[i])

    def issue_wo(q):
        for s in range(SB):
            i = slot(Q_WO + q, s)
            put(wo.at[:, pl.ds((q * SB + s) * COLS, COLS)], ring.at[i], sem.at[i])

    def issue_gu(ref, nb, quad):
        for s in range(SB):
            i = slot(quad, s)
            cols = pl.ds(nb * COLS if isinstance(nb, int) else pl.multiple_of(nb * COLS, COLS), COLS)
            put(ref.at[pl.ds(s * ROWS, ROWS), cols], ring.at[i], sem.at[i])

    def issue_wd(nb):
        cols = pl.ds(nb * COLS if isinstance(nb, int) else pl.multiple_of(nb * COLS, COLS), COLS)
        for s in range(SB):
            i = slot(Q_WD + nb, s)
            if s < 3:
                put(wd.at[pl.ds(s * ROWS, ROWS), cols], ring.at[i], sem.at[i])
            else:
                put(wd.at[pl.ds(s * ROWS, FF - 3 * ROWS), cols], ring.at[i, pl.ds(0, FF - 3 * ROWS), :], sem.at[i])

    def issue(quad):
        if quad < Q_K0:
            issue_wq(quad)
        elif quad == Q_K0:
            issue_kv(k_hbm, 0, quad)
        elif quad < Q_VL:
            g = (quad - Q_KV) // 2
            if (quad - Q_KV) % 2 == 0:
                issue_kv(k_hbm, g + 1, quad)
            else:
                issue_kv(v_hbm, g, quad)
        elif quad == Q_VL:
            issue_kv(v_hbm, GROUPS - 1, quad)
        elif quad < Q_GU:
            issue_wo(quad - Q_WO)
        elif quad < Q_WD:
            n = quad - Q_GU
            issue_gu(wg if n % 2 == 0 else wu, n // 2, quad)
        elif quad < Q_WD + NB:
            issue_wd(quad - Q_WD)

    def arrive(quad, s, rows=ROWS):
        i = slot(quad, s)
        pltpu.make_async_copy(wq.at[pl.ds(0, rows), pl.ds(0, COLS)], ring.at[i, pl.ds(0, rows), :], sem.at[i]).wait()

    xcopies = [pltpu.make_async_copy(x_hbm.at[:, pl.ds(j * TILE, TILE)], xb.at[j], xsem.at[j]) for j in range(NT)]
    small = [pltpu.make_async_copy(a, b, gsem.at[n]) for n, (a, b) in enumerate(
        ((ga_hbm, gb.at[0]), (gm_hbm, gb.at[1]), (rot_hbm, rb)))]
    for c in xcopies + small:
        c.start()
    for quad in range(R):
        issue(quad)

    barrier = pltpu.get_barrier_semaphore()
    for peer in (sib, far):
        pl.semaphore_signal(barrier, inc=1, device_id={"tp": peer}, device_id_type=pl.DeviceIdType.MESH)

    for c in xcopies + small:
        c.wait()

    def normed(src, gain):
        total = jnp.zeros((BATCH, 128), F32)
        for j in range(NT):
            t = src(j).astype(F32)
            t = t * t
            total += t[:, :128] + t[:, 128:]
        scale = lax.rsqrt(jnp.sum(total, -1, keepdims=True) * (1.0 / D) + 1e-6)
        g = gb[gain].astype(F32)
        for j in range(NT):
            t = src(j).astype(F32)
            row = jnp.concatenate([g[2 * j:2 * j + 1], g[2 * j + 1:2 * j + 2]], 1)
            ab[j] = (t * scale * row).astype(BF16)

    def lhs(kc):
        return jnp.concatenate([ab[kc * 4 + t] for t in range(4)], 1)

    def dot(a, b):
        return jnp.dot(a, b, preferred_element_type=F32)

    normed(lambda j: xb[j], 0)

    cos, sin = rb[0:1, :], rb[1:2, :]
    for nc in range(2):
        for s in range(SB):
            arrive(nc, s)
        for n in range(2):
            acc = None
            for kc in range(4):
                d = dot(lhs(kc), ring[slot(nc, kc), :, n * TILE:(n + 1) * TILE])
                acc = d if acc is None else acc + d
            for hh in range(2):
                t = acc[:, hh * HEAD:(hh + 1) * HEAD].astype(BF16).astype(F32)
                r = t * cos + pltpu.roll(t, HEAD // 2, 1) * sin
                head = nc * 4 + n * 2 + hh
                qb[head * BATCH:(head + 1) * BATCH, :] = r.astype(BF16).astype(F32)
        issue(R + nc)

    row = lax.broadcasted_iota(jnp.int32, (8, 128), 0)
    lane = lax.broadcasted_iota(jnp.int32, (8, 128), 1)
    mine = (lane % 2) == (row // 4)
    zero = jnp.zeros((8, HEAD), F32)
    rate = HEAD**-0.5 * float(np.log2(np.e))

    def scores(g, quad, sc):
        for s in range(SB):
            q = qb[pl.ds(g * SB + s, 8, stride=BATCH), :]
            qq = jnp.concatenate([jnp.concatenate([q, zero], 1), jnp.concatenate([zero, q], 1)], 0).astype(BF16)
            i = slot(quad, s)
            for h in range(2):
                sc[s, h] = lax.dot_general(qq, ring[i, :, h * TILE:(h + 1) * TILE], (((1,), (1,)), ((), ())),
                                           preferred_element_type=F32)

    def attend(g, quad, sc):
        for s in range(SB):
            i = slot(quad, s)
            p = {}
            top = None
            for h in range(2):
                for r in range(2):
                    for c in range(ROWS // 128):
                        t = jnp.where(mine, sc[s, h, r * 8:(r + 1) * 8, c * 128:(c + 1) * 128], NEG)
                        p[h, r, c] = t
                        top = t if top is None else jnp.maximum(top, t)
            top = jnp.max(top, -1, keepdims=True)
            total = None
            for key, t in p.items():
                e = jnp.exp2((t - top) * rate)
                p[key] = e
                total = e if total is None else total + e
            inv = 1.0 / jnp.sum(total, -1, keepdims=True)
            o = None
            for h in range(2):
                w = jnp.concatenate([jnp.concatenate([p[h, r, c] * inv for c in range(ROWS // 128)], 1)
                                     for r in range(2)], 0).astype(BF16)
                d = dot(w, ring[i, :, h * TILE:(h + 1) * TILE])
                o = d if o is None else o + d
            o = o[0:8, 0:HEAD] + o[8:16, HEAD:TILE]
            seen[pl.ds(g * SB + s, 8, stride=BATCH), :] = o.astype(BF16).astype(F32)

    for s in range(SB):
        arrive(Q_K0, s)
    scores(0, Q_K0, sca)
    issue(R + Q_K0)

    def half(g, read, write):
        kq, vq = Q_KV + 2 * g, Q_KV + 1 + 2 * g
        for s in range(SB):
            arrive(kq, s)
            arrive(vq, s)
        scores(g + 1, kq, write)
        attend(g, vq, read)

    def pair(gp, _):
        for e, (read, write) in enumerate(((sca, scb), (scb, sca))):
            g = 2 * gp + e
            half(g, read, write)
            last = (Q_VL - R - Q_KV) // 2

            @pl.when(g < last)
            def _():
                issue_kv(k_hbm, g + 1 + R // 2, Q_KV + 2 * g + R)
                issue_kv(v_hbm, g + R // 2, Q_KV + 1 + 2 * g + R)

            for n in range(last, GROUPS - 2):
                if n % 2 == e:
                    @pl.when(g == n)
                    def _(n=n):
                        issue(Q_KV + 2 * n + R)
                        issue(Q_KV + 1 + 2 * n + R)
        return 0

    lax.fori_loop(0, GROUPS // 2 - 1, pair, 0)
    half(GROUPS - 2, sca, scb)
    issue(Q_KV + 2 * (GROUPS - 2) + R)
    issue(Q_KV + 1 + 2 * (GROUPS - 2) + R)
    for s in range(SB):
        arrive(Q_VL, s)
    attend(GROUPS - 1, Q_VL, scb)
    issue(Q_VL + R)

    def remote(src, dst, a, b, peer):
        return pltpu.make_async_remote_copy(src_ref=src, dst_ref=dst, send_sem=a, recv_sem=b, device_id={"tp": peer},
                                            device_id_type=pl.DeviceIdType.MESH)

    def copy1(e, c):
        return remote(s1.at[e, c, 1 - k], r1.at[e, c], ss1.at[e, c], rs1.at[e, c], sib)

    def copy2(e, c):
        return remote(s2.at[e, c], r2.at[e, c], ss2.at[e, c], rs2.at[e, c], far)

    def copy3(e, c):
        return remote(y.at[e, 2 * c + k], y.at[e, 2 * c + k], ss3.at[e, c], rs3.at[e, c], sib)

    def write(c, which):
        j = 2 * c + which
        cols = pl.ds(pl.multiple_of(j * TILE, TILE), TILE)
        return pltpu.make_async_copy(y.at[1, j], out.at[:, cols], osem.at[j])

    def stage1(e, c, tiles):
        for n in range(2):
            f1[c, n] = tiles[n]
            s1[e, c, n] = tiles[n].astype(BF16)
        copy1(e, c).start()

    def stage2(e, c):
        copy1(e, c).wait_recv()
        s2[e, c] = (f1[c, k] + r1[e, c].astype(F32)).astype(BF16)
        copy2(e, c).start()

    def stage3(e, c):
        copy2(e, c).wait_recv()
        j = 2 * c + k
        base = (xb[j] if e == 0 else y[0, j]).astype(F32)
        y[e, j] = (base + (s2[e, c].astype(F32) + r2[e, c].astype(F32))).astype(BF16)
        copy3(e, c).start()
        if e == 1:
            write(c, k).start()

    def stage4(e, c):
        copy3(e, c).wait_recv()
        if e == 1:
            write(c, 1 - k).start()

    def behind(e, c):
        @pl.when(c >= 1)
        def _():
            stage2(e, c - 1)

        @pl.when(c >= 3)
        def _():
            stage3(e, c - 3)

    def drain(e):
        stage2(e, NB - 1)
        for c in range(NB - 3, NB):
            stage3(e, c)
        for c in range(NB):
            stage4(e, c)

    def sent(e):
        for c in range(NB):
            copy1(e, c).wait_send()
            copy2(e, c).wait_send()
            copy3(e, c).wait_send()

    pl.semaphore_wait(barrier, 2)

    def wo_step(c, _):
        arrive(Q_WO + c // SB, lax.rem(c, SB))
        i = slot(Q_WO + c // SB, lax.rem(c, SB))
        a = jnp.concatenate([seen[h * BATCH:(h + 1) * BATCH, :].astype(BF16) for h in range(8)], 1)
        stage1(0, c, [dot(a, ring[i, :, n * TILE:(n + 1) * TILE]) for n in range(2)])
        behind(0, c)
        return 0

    lax.fori_loop(0, NB, wo_step, 0)
    issue(Q_WO + R)
    issue(Q_WO + 1 + R)
    drain(0)
    normed(lambda j: y[0, j], 1)

    def gu_step(nb, _):
        gq, uq = Q_GU + 2 * nb, Q_GU + 1 + 2 * nb
        for s in range(SB):
            arrive(gq, s)
            arrive(uq, s)
        for n in range(2):
            cols = slice(n * TILE, (n + 1) * TILE)
            gate = up = None
            for kc in range(4):
                d = dot(lhs(kc), ring[slot(gq, kc), :, cols])
                gate = d if gate is None else gate + d
            for kc in range(4):
                d = dot(lhs(kc), ring[slot(uq, kc), :, cols])
                up = d if up is None else up + d
            hid[nb, :, cols] = (jax.nn.silu(gate) * up).astype(BF16)
        for n in range(NF):
            if Q_GU + 2 * n + R < Q_WD + NB:
                @pl.when(nb == n)
                def _(n=n):
                    issue(Q_GU + 2 * n + R)
                    issue(Q_GU + 1 + 2 * n + R)
        return 0

    lax.fori_loop(0, NF, gu_step, 0)

    def wd_step(c, _):
        for s in range(3):
            arrive(Q_WD + c, s)
        arrive(Q_WD + c, 3, FF - 3 * ROWS)
        tiles = []
        for n in range(2):
            cols = slice(n * TILE, (n + 1) * TILE)
            acc = None
            for kc in range(4):
                i = slot(Q_WD + c, kc)
                if kc < 3:
                    d = dot(jnp.concatenate([hid[2 * kc], hid[2 * kc + 1]], 1), ring[i, :, cols])
                else:
                    d = dot(hid[NF - 1], ring[i, 0:FF - 3 * ROWS, cols])
                acc = d if acc is None else acc + d
            tiles.append(acc)
        stage1(1, c, tiles)
        behind(1, c)
        return 0

    lax.fori_loop(0, NB, wd_step, 0)
    drain(1)
    sent(0)
    sent(1)
    for c in range(NB):
        for n in range(2):
            write(c, n).wait()


def solution(mesh):
    half = HEAD // 2
    angle = (CACHE - 1) * float(THETA) ** (-np.arange(half) / half)
    turn = np.zeros((8, HEAD), np.float32)
    turn[0] = np.concatenate([np.cos(angle), np.cos(angle)])
    turn[1] = np.concatenate([-np.sin(angle), np.sin(angle)])
    hbm = pl.BlockSpec(memory_space=pl.ANY)

    def step(x, k_cache, v_cache, gain_a, wq, wo, gain_m, w_gate, w_up, w_down):
        flat = (BATCH, CACHE * KV, HEAD)
        dma = pltpu.SemaphoreType.DMA
        call = pl.pallas_call(
            kernel,
            out_shape=jax.ShapeDtypeStruct((BATCH, D), BF16),
            in_specs=[hbm] * 11,
            out_specs=hbm,
            scratch_shapes=[
                pltpu.VMEM((R * SB, ROWS, COLS), BF16),
                pltpu.VMEM((NT, BATCH, TILE), BF16),
                pltpu.VMEM((NT, BATCH, TILE), BF16),
                pltpu.VMEM((2, D // 128, 128), BF16),
                pltpu.VMEM((8, HEAD), F32),
                pltpu.VMEM((8 * BATCH, HEAD), F32),
                pltpu.VMEM((SB, 2, 16, ROWS), F32),
                pltpu.VMEM((SB, 2, 16, ROWS), F32),
                pltpu.VMEM((8 * BATCH, HEAD), F32),
                pltpu.VMEM((NF, BATCH, COLS), BF16),
                pltpu.VMEM((NB, 2, BATCH, TILE), F32),
                pltpu.VMEM((2, NB, 2, BATCH, TILE), BF16),
                pltpu.VMEM((2, NB, BATCH, TILE), BF16),
                pltpu.VMEM((2, NB, BATCH, TILE), BF16),
                pltpu.VMEM((2, NB, BATCH, TILE), BF16),
                pltpu.VMEM((2, NT, BATCH, TILE), BF16),
                dma((R * SB,)), dma((NT,)), dma((3,)),
                dma((2, NB)), dma((2, NB)), dma((2, NB)), dma((2, NB)), dma((2, NB)), dma((2, NB)), dma((NT,)),
            ],
            compiler_params=pltpu.CompilerParams(collective_id=0, has_side_effects=True, vmem_limit_bytes=67_000_000),
            cost_estimate=pl.CostEstimate(flops=20 * 10**9, bytes_accessed=240 * 10**6, transcendentals=0),
            name="layer",
        )
        return call(x, k_cache.reshape(flat), v_cache.reshape(flat), gain_a.reshape(D // 128, 128), wq, wo,
                    gain_m.reshape(D // 128, 128), w_gate, w_up, w_down, jnp.asarray(turn))

    states, cache, columns, rows_of = P("dp", None), P("dp", None, "tp", None), P(None, "tp"), P("tp", None)
    return jax.shard_map(
        step,
        mesh=mesh,
        in_specs=(states, cache, cache, P(None), columns, rows_of, P(None), columns, columns, rows_of),
        out_specs=states,
        check_vma=False,
    )
```

time: 186 us -> 90.3 us (0.49)
  matrix products: 108 us -> 0 us
  Pallas kernels: 0 us -> 88.3 us
  waiting for transfers between devices: 58.4 us -> 0 us
  between operations: 13.5 us -> 0.01 us
  other arithmetic: 5.43 us -> 0 us
    pallas_call x0 -> x1, Pallas kernels: none -> 88.3 us  [step(): call(x, k_cache.reshape(flat), v_cache.reshape(flat), gain_a.reshape(D //...]
    dot_general x5 -> x0, matrix products: 72.5 us -> none  [the longest x1 26.6 us: einsum(): return jnp.einsum(form, a.astype(jnp.float32), b.astype(jnp.float32))]
    psum x2 -> x0, waiting for transfers between devices: 58.4 us -> none  [added(): lax.psum(term.astype(jnp.bfloat16), 'tp').astype(jnp.float32)]
    sub x1 -> x0, matrix products: 35.4 us -> none  [seen_by(): weights = jax.nn.softmax(scores, -1).astype(jnp.bfloat16)]
    convert_element_type x3 -> x0, other arithmetic: 2.66 us -> none  [the longest x1 1.96 us: added(): (t.astype(jnp.float32) + lax.psum(term.astype(jnp.bfloat16), 'tp').astype...]
    reduce_sum x2 -> x0, other arithmetic: 2.57 us -> none  [normed(): scale = lax.rsqrt(jnp.mean(wide * wide, -1, keepdims=True) + 1e-06)]
  transfers between devices with their start and end apart: 2 -> 0, of which waited for: 2 -> 0; matrix products, arithmetic and copies ran while one was open for 0% -> 0% of each run, Pallas kernels for 0% -> 0%
where the time goes in v1:
time: 90.3 us; the launch traced here: 90.2 us
  Pallas kernels  88.3 us (98%)
  local copies, waits for them, and re-layouts  1.87 us (2%)
    pallas_call x1, Pallas kernels, step(): call(x, k_cache.reshape(flat), v_cache.reshape(flat), gain_a.reshape(D //...  88.3 us
    unnamed x1, local copies, waits for them, and re-layouts  1.87 us

profile of v1, /device:TPU:0, one launch (start us, length us, event | category | flops | bytes accessed | tf_op | source)
XLA Modules:
  0.0 90.2 jit_solution(16925801657790321142)
XLA Ops:
  0.0 88.3 %layer.1 = bf16[64,4096]{1,0:T(8,128)(2,1)} custom-call(bf16[64,4096]{1,0:T(8,128)(2,1)} %x_hbm.1, bf16[64,4096,128]{2,1,0:T(8,128)(2,1)} %bitcast.k_hbm, bf16[64,4096,128]{2,1,0:T(8,128)(2,1)} %bitcast.1.v_hbm, bf16[32,128]{1,0:T(8,128)(2,1)} %bitcast.4, bf16[4096,1024]{1,0:T(8,128)(2,1)} %wq.1, bf16[1024,4096]{1,0:T(8,128)(2,1)} %wo.1, ...), custom_call_target="tpu_custom_call" | custom-call | flops 20000000000 | bytes 240000000 | tf_op jit(solution)/shard_map/layer/pallas_call | solution.py:409
  88.3 1.9 %copy.13 = bf16[64,4096]{1,0:T(8,128)(2,1)} copy(bf16[64,4096]{1,0:T(8,128)(2,1)} %layer.1) | data formatting | bytes 1048576

commit v2 on v1

--- a/solution.py
+++ b/solution.py
@@ -15,20 +15,21 @@
 FF = 3584
 ROWS, COLS = 1024, 512
 SB = 4
-R = 12
+R = 11
+HALF = BATCH // 2
 GROUPS = BATCH // SB
 TILE = 256
 NT = D // TILE
 NB = D // COLS
 NF = FF // COLS
-Q_K0, Q_KV, Q_VL, Q_WO, Q_GU, Q_WD = 2, 3, 33, 34, 36, 50
+Q_K0, Q_KV, Q_VL, Q_GU, Q_WD = 0, 1, 31, 32, 46
 F32, BF16 = jnp.float32, jnp.bfloat16
 NEG = float("-inf")
 
 
 def kernel(x_hbm, k_hbm, v_hbm, ga_hbm, wq, wo, gm_hbm, wg, wu, wd, rot_hbm, out,
-           ring, xb, ab, gb, rb, qb, sca, scb, seen, hid, f1, s1, r1, s2, r2, y,
-           sem, xsem, gsem, ss1, rs1, ss2, rs2, ss3, rs3, osem):
+           ring, held, xb, ab, gb, rb, qb, sca, scb, seen, hid, f1, s1, r1, s2, r2, y,
+           sem, wsem, xsem, gsem, ss1, rs1, ss2, rs2, ss3, rs3):
     tp = lax.axis_index("tp")
     k = lax.rem(tp, 2)
     sib = tp + 1 - 2 * k
@@ -38,12 +39,11 @@
         return (quad % R if isinstance(quad, int) else lax.rem(quad, R)) * SB + s
 
     def put(src, dst, s):
-        pltpu.make_async_copy(src, dst, s).start()
-
-    def issue_wq(nc):
-        for s in range(SB):
-            i = slot(nc, s)
-            put(wq.at[pl.ds(s * ROWS, ROWS), pl.ds(nc * COLS, COLS)], ring.at[i], sem.at[i])
+        pltpu.make_async_copy(src, dst, s).start(priority=1)
+
+    def issue_wq():
+        for i in range(2 * SB):
+            pltpu.make_async_copy(wq.at[pl.ds(i % SB * ROWS, ROWS), pl.ds(i // SB * COLS, COLS)], held.at[i], wsem.at[i]).start()
 
     def issue_kv(ref, g, quad):
         for s in range(SB):
@@ -51,10 +51,9 @@
             for c in range(4):
                 put(ref.at[g * SB + s, pl.ds(c * ROWS, ROWS), :], ring.at[i, :, pl.ds(c * 128, 128)], sem.at[i])
 
-    def issue_wo(q):
-        for s in range(SB):
-            i = slot(Q_WO + q, s)
-            put(wo.at[:, pl.ds((q * SB + s) * COLS, COLS)], ring.at[i], sem.at[i])
+    def issue_wo():
+        for i in range(NB):
+            put(wo.at[:, pl.ds(i * COLS, COLS)], held.at[i], wsem.at[i])
 
     def issue_gu(ref, nb, quad):
         for s in range(SB):
@@ -72,9 +71,7 @@
                 put(wd.at[pl.ds(s * ROWS, FF - 3 * ROWS), cols], ring.at[i, pl.ds(0, FF - 3 * ROWS), :], sem.at[i])
 
     def issue(quad):
-        if quad < Q_K0:
-            issue_wq(quad)
-        elif quad == Q_K0:
+        if quad == Q_K0:
             issue_kv(k_hbm, 0, quad)
         elif quad < Q_VL:
             g = (quad - Q_KV) // 2
@@ -84,8 +81,6 @@
                 issue_kv(v_hbm, g, quad)
         elif quad == Q_VL:
             issue_kv(v_hbm, GROUPS - 1, quad)
-        elif quad < Q_GU:
-            issue_wo(quad - Q_WO)
         elif quad < Q_WD:
             n = quad - Q_GU
             issue_gu(wg if n % 2 == 0 else wu, n // 2, quad)
@@ -96,11 +91,15 @@
         i = slot(quad, s)
         pltpu.make_async_copy(wq.at[pl.ds(0, rows), pl.ds(0, COLS)], ring.at[i, pl.ds(0, rows), :], sem.at[i]).wait()
 
+    def held_arrive(i):
+        pltpu.make_async_copy(wq.at[pl.ds(0, ROWS), pl.ds(0, COLS)], held.at[i], wsem.at[i]).wait()
+
     xcopies = [pltpu.make_async_copy(x_hbm.at[:, pl.ds(j * TILE, TILE)], xb.at[j], xsem.at[j]) for j in range(NT)]
     small = [pltpu.make_async_copy(a, b, gsem.at[n]) for n, (a, b) in enumerate(
         ((ga_hbm, gb.at[0]), (gm_hbm, gb.at[1]), (rot_hbm, rb)))]
     for c in xcopies + small:
         c.start()
+    issue_wq()
     for quad in range(R):
         issue(quad)
 
@@ -135,18 +134,18 @@
     cos, sin = rb[0:1, :], rb[1:2, :]
     for nc in range(2):
         for s in range(SB):
-            arrive(nc, s)
+            held_arrive(nc * SB + s)
         for n in range(2):
             acc = None
             for kc in range(4):
-                d = dot(lhs(kc), ring[slot(nc, kc), :, n * TILE:(n + 1) * TILE])
+                d = dot(lhs(kc), held[nc * SB + kc, :, n * TILE:(n + 1) * TILE])
                 acc = d if acc is None else acc + d
             for hh in range(2):
                 t = acc[:, hh * HEAD:(hh + 1) * HEAD].astype(BF16).astype(F32)
                 r = t * cos + pltpu.roll(t, HEAD // 2, 1) * sin
                 head = nc * 4 + n * 2 + hh
                 qb[head * BATCH:(head + 1) * BATCH, :] = r.astype(BF16).astype(F32)
-        issue(R + nc)
+    issue_wo()
 
     row = lax.broadcasted_iota(jnp.int32, (8, 128), 0)
     lane = lax.broadcasted_iota(jnp.int32, (8, 128), 1)
@@ -190,6 +189,86 @@
             o = o[0:8, 0:HEAD] + o[8:16, HEAD:TILE]
             seen[pl.ds(g * SB + s, 8, stride=BATCH), :] = o.astype(BF16).astype(F32)
 
+    def rows(e):
+        return pl.ds(0, BATCH if e == 2 else HALF)
+
+    def place(e):
+        return (1, pl.ds(0, BATCH)) if e == 2 else (0, pl.ds(e * HALF, HALF))
+    def remote(src, dst, a, b, peer):
+        return pltpu.make_async_remote_copy(src_ref=src, dst_ref=dst, send_sem=a, recv_sem=b, device_id={"tp": peer},
+                                            device_id_type=pl.DeviceIdType.MESH)
+
+    def copy1(e, c):
+        return remote(s1.at[e, c, 1 - k, rows(e)], r1.at[e, c, rows(e)], ss1.at[e, c], rs1.at[e, c], sib)
+
+    def copy2(e, c):
+        return remote(s2.at[e, c, rows(e)], r2.at[e, c, rows(e)], ss2.at[e, c], rs2.at[e, c], far)
+
+    def copy3(e, c):
+        which, at = place(e)
+        return remote(y.at[which, 2 * c + k, at], y.at[which, 2 * c + k, at], ss3.at[e, c], rs3.at[e, c], sib)
+
+    def stage1(e, c, tiles):
+        for n in range(2):
+            f1[c, n, rows(e)] = tiles[n]
+            s1[e, c, n, rows(e)] = tiles[n].astype(BF16)
+        copy1(e, c).start()
+
+    def stage2(e, c):
+        copy1(e, c).wait_recv()
+        s2[e, c, rows(e)] = (f1[c, k, rows(e)] + r1[e, c, rows(e)].astype(F32)).astype(BF16)
+        copy2(e, c).start()
+
+    def stage3(e, c):
+        copy2(e, c).wait_recv()
+        j = 2 * c + k
+        which, at = place(e)
+        base = (y[0, j] if e == 2 else xb[j, at]).astype(F32)
+        y[which, j, at] = (base + (s2[e, c, rows(e)].astype(F32) + r2[e, c, rows(e)].astype(F32))).astype(BF16)
+        copy3(e, c).start()
+
+    def stage4(e, c):
+        copy3(e, c).wait_recv()
+        if e == 2:
+            for j in (2 * c, 2 * c + 1):
+                out[:, j * TILE:(j + 1) * TILE] = y[1, j]
+
+    def behind(e, c):
+        @pl.when(c >= 2)
+        def _():
+            stage2(e, c - 2)
+
+        @pl.when(c >= 5)
+        def _():
+            stage3(e, c - 5)
+
+    def drain(e):
+        for c in range(NB - 2, NB):
+            stage2(e, c)
+        for c in range(NB - 5, NB):
+            stage3(e, c)
+        for c in range(NB):
+            stage4(e, c)
+
+    def sent(e):
+        for c in range(NB):
+            copy1(e, c).wait_send()
+            copy2(e, c).wait_send()
+            copy3(e, c).wait_send()
+
+    def loop(body):
+        def one(c, _):
+            body(c)
+            return 0
+        lax.fori_loop(0, NB, one, 0)
+
+    def wo_steps(e):
+        def one(c):
+            at = e * HALF
+            a = jnp.concatenate([seen[h * BATCH + at:h * BATCH + at + HALF, :].astype(BF16) for h in range(8)], 1)
+            stage1(e, c, [dot(a, held[c, :, n * TILE:(n + 1) * TILE]) for n in range(2)])
+        loop(one)
+
     for s in range(SB):
         arrive(Q_K0, s)
     scores(0, Q_K0, sca)
@@ -211,8 +290,12 @@
 
             @pl.when(g < last)
             def _():
-                issue_kv(k_hbm, g + 1 + R // 2, Q_KV + 2 * g + R)
-                issue_kv(v_hbm, g + R // 2, Q_KV + 1 + 2 * g + R)
+                if R % 2 == 0:
+                    issue_kv(k_hbm, g + 1 + R // 2, Q_KV + 2 * g + R)
+                    issue_kv(v_hbm, g + R // 2, Q_KV + 1 + 2 * g + R)
+                else:
+                    issue_kv(v_hbm, g + R // 2, Q_KV + 2 * g + R)
+                    issue_kv(k_hbm, g + 2 + R // 2, Q_KV + 1 + 2 * g + R)
 
             for n in range(last, GROUPS - 2):
                 if n % 2 == e:
@@ -220,6 +303,21 @@
                     def _(n=n):
                         issue(Q_KV + 2 * n + R)
                         issue(Q_KV + 1 + 2 * n + R)
+
+        @pl.when(gp == GROUPS // 4 - 1)
+        def _():
+            pl.semaphore_wait(barrier, 2)
+            for i in range(NB):
+                held_arrive(i)
+            wo_steps(0)
+
+        @pl.when(gp == GROUPS // 4)
+        def _():
+            loop(lambda c: stage2(0, c))
+
+        @pl.when(gp == GROUPS // 4 + 1)
+        def _():
+            loop(lambda c: stage3(0, c))
         return 0
 
     lax.fori_loop(0, GROUPS // 2 - 1, pair, 0)
@@ -231,85 +329,12 @@
     attend(GROUPS - 1, Q_VL, scb)
     issue(Q_VL + R)
 
-    def remote(src, dst, a, b, peer):
-        return pltpu.make_async_remote_copy(src_ref=src, dst_ref=dst, send_sem=a, recv_sem=b, device_id={"tp": peer},
-                                            device_id_type=pl.DeviceIdType.MESH)
-
-    def copy1(e, c):
-        return remote(s1.at[e, c, 1 - k], r1.at[e, c], ss1.at[e, c], rs1.at[e, c], sib)
-
-    def copy2(e, c):
-        return remote(s2.at[e, c], r2.at[e, c], ss2.at[e, c], rs2.at[e, c], far)
-
-    def copy3(e, c):
-        return remote(y.at[e, 2 * c + k], y.at[e, 2 * c + k], ss3.at[e, c], rs3.at[e, c], sib)
-
-    def write(c, which):
-        j = 2 * c + which
-        cols = pl.ds(pl.multiple_of(j * TILE, TILE), TILE)
-        return pltpu.make_async_copy(y.at[1, j], out.at[:, cols], osem.at[j])
-
-    def stage1(e, c, tiles):
-        for n in range(2):
-            f1[c, n] = tiles[n]
-            s1[e, c, n] = tiles[n].astype(BF16)
-        copy1(e, c).start()
-
-    def stage2(e, c):
-        copy1(e, c).wait_recv()
-        s2[e, c] = (f1[c, k] + r1[e, c].astype(F32)).astype(BF16)
-        copy2(e, c).start()
-
-    def stage3(e, c):
-        copy2(e, c).wait_recv()
-        j = 2 * c + k
-        base = (xb[j] if e == 0 else y[0, j]).astype(F32)
-        y[e, j] = (base + (s2[e, c].astype(F32) + r2[e, c].astype(F32))).astype(BF16)
-        copy3(e, c).start()
-        if e == 1:
-            write(c, k).start()
-
-    def stage4(e, c):
-        copy3(e, c).wait_recv()
-        if e == 1:
-            write(c, 1 - k).start()
-
-    def behind(e, c):
-        @pl.when(c >= 1)
-        def _():
-            stage2(e, c - 1)
-
-        @pl.when(c >= 3)
-        def _():
-            stage3(e, c - 3)
-
-    def drain(e):
-        stage2(e, NB - 1)
-        for c in range(NB - 3, NB):
-            stage3(e, c)
+    wo_steps(1)
+    loop(lambda c: stage2(1, c))
+    loop(lambda c: stage3(1, c))
+    for e in range(2):
         for c in range(NB):
             stage4(e, c)
-
-    def sent(e):
-        for c in range(NB):
-            copy1(e, c).wait_send()
-            copy2(e, c).wait_send()
-            copy3(e, c).wait_send()
-
-    pl.semaphore_wait(barrier, 2)
-
-    def wo_step(c, _):
-        arrive(Q_WO + c // SB, lax.rem(c, SB))
-        i = slot(Q_WO + c // SB, lax.rem(c, SB))
-        a = jnp.concatenate([seen[h * BATCH:(h + 1) * BATCH, :].astype(BF16) for h in range(8)], 1)
-        stage1(0, c, [dot(a, ring[i, :, n * TILE:(n + 1) * TILE]) for n in range(2)])
-        behind(0, c)
-        return 0
-
-    lax.fori_loop(0, NB, wo_step, 0)
-    issue(Q_WO + R)
-    issue(Q_WO + 1 + R)
-    drain(0)
     normed(lambda j: y[0, j], 1)
 
     def gu_step(nb, _):
@@ -353,17 +378,15 @@
                     d = dot(hid[NF - 1], ring[i, 0:FF - 3 * ROWS, cols])
                 acc = d if acc is None else acc + d
             tiles.append(acc)
-        stage1(1, c, tiles)
-        behind(1, c)
+        stage1(2, c, tiles)
+        behind(2, c)
         return 0
 
-    lax.fori_loop(0, NB, wd_step, 0)
-    drain(1)
     sent(0)
     sent(1)
-    for c in range(NB):
-        for n in range(2):
-            write(c, n).wait()
+    lax.fori_loop(0, NB, wd_step, 0)
+    drain(2)
+    sent(2)
 
 
 def solution(mesh):
@@ -379,11 +402,12 @@
         dma = pltpu.SemaphoreType.DMA
         call = pl.pallas_call(
             kernel,
-            out_shape=jax.ShapeDtypeStruct((BATCH, D), BF16),
+            out_shape=pltpu.VMEM((BATCH, D), BF16),
             in_specs=[hbm] * 11,
-            out_specs=hbm,
+            out_specs=pl.BlockSpec(memory_space=pltpu.VMEM),
             scratch_shapes=[
                 pltpu.VMEM((R * SB, ROWS, COLS), BF16),
+                pltpu.VMEM((NB, ROWS, COLS), BF16),
                 pltpu.VMEM((NT, BATCH, TILE), BF16),
                 pltpu.VMEM((NT, BATCH, TILE), BF16),
                 pltpu.VMEM((2, D // 128, 128), BF16),
@@ -394,15 +418,15 @@
                 pltpu.VMEM((8 * BATCH, HEAD), F32),
                 pltpu.VMEM((NF, BATCH, COLS), BF16),
                 pltpu.VMEM((NB, 2, BATCH, TILE), F32),
-                pltpu.VMEM((2, NB, 2, BATCH, TILE), BF16),
-                pltpu.VMEM((2, NB, BATCH, TILE), BF16),
-                pltpu.VMEM((2, NB, BATCH, TILE), BF16),
-                pltpu.VMEM((2, NB, BATCH, TILE), BF16),
+                pltpu.VMEM((3, NB, 2, BATCH, TILE), BF16),
+                pltpu.VMEM((3, NB, BATCH, TILE), BF16),
+                pltpu.VMEM((3, NB, BATCH, TILE), BF16),
+                pltpu.VMEM((3, NB, BATCH, TILE), BF16),
                 pltpu.VMEM((2, NT, BATCH, TILE), BF16),
-                dma((R * SB,)), dma((NT,)), dma((3,)),
-                dma((2, NB)), dma((2, NB)), dma((2, NB)), dma((2, NB)), dma((2, NB)), dma((2, NB)), dma((NT,)),
+                dma((R * SB,)), dma((NB,)), dma((NT,)), dma((3,)),
+                *[dma((3, NB))] * 6,
             ],
-            compiler_params=pltpu.CompilerParams(collective_id=0, has_side_effects=True, vmem_limit_bytes=67_000_000),
+            compiler_params=pltpu.CompilerParams(collective_id=0, has_side_effects=True, vmem_limit_bytes=65_900_000),
             cost_estimate=pl.CostEstimate(flops=20 * 10**9, bytes_accessed=240 * 10**6, transcendentals=0),
             name="layer",
         )

time: 90.3 us -> 82.1 us (0.909)
  Pallas kernels: 88.3 us -> 81.2 us
  local copies, waits for them, and re-layouts: 1.87 us -> 0.8 us
    pallas_call x1, Pallas kernels: 88.3 us -> 81.2 us  [step(): call(x, k_cache.reshape(flat), v_cache.reshape(flat), gain_a.reshape(D //...]
    unnamed x1, local copies, waits for them, and re-layouts: 1.87 us -> 0.8 us
where the time goes in v2:
time: 82.1 us; the launch traced here: 82 us
  Pallas kernels  81.2 us (99%)
    pallas_call x1, Pallas kernels, step(): call(x, k_cache.reshape(flat), v_cache.reshape(flat), gain_a.reshape(D //...  81.2 us

profile of v2, /device:TPU:0, one launch (start us, length us, event | category | flops | bytes accessed | tf_op | source)
XLA Modules:
  0.0 82.0 jit_solution(9028855561713967948)
XLA Ops:
  0.0 81.2 %layer.1 = bf16[64,4096]{1,0:T(8,128)(2,1)S(1)} custom-call(bf16[64,4096]{1,0:T(8,128)(2,1)} %x_hbm.1, bf16[64,4096,128]{2,1,0:T(8,128)(2,1)} %bitcast.k_hbm, bf16[64,4096,128]{2,1,0:T(8,128)(2,1)} %bitcast.1.v_hbm, bf16[32,128]{1,0:T(8,128)(2,1)} %bitcast.4, bf16[4096,1024]{1,0:T(8,128)(2,1)} %wq.1, bf16[1024,4096]{1,0:T(8,128)(2,1)} %wo.1, ...), custom_call_target="tpu_custom_call" | custom-call | flops 20000000000 | bytes 240000000 | tf_op jit(solution)/shard_map/layer/pallas_call | solution.py:433
  81.2 0.8 copy.13

commit v3 on v2

--- a/solution.py
+++ b/solution.py
@@ -16,7 +16,7 @@
 ROWS, COLS = 1024, 512
 SB = 4
 R = 11
-HALF = BATCH // 2
+EARLY = 48
 GROUPS = BATCH // SB
 TILE = 256
 NT = D // TILE
@@ -29,7 +29,7 @@
 
 def kernel(x_hbm, k_hbm, v_hbm, ga_hbm, wq, wo, gm_hbm, wg, wu, wd, rot_hbm, out,
            ring, held, xb, ab, gb, rb, qb, sca, scb, seen, hid, f1, s1, r1, s2, r2, y,
-           sem, wsem, xsem, gsem, ss1, rs1, ss2, rs2, ss3, rs3):
+           fz, sz, rz, yz, sem, wsem, lsem, xsem, gsem, xs, xr):
     tp = lax.axis_index("tp")
     k = lax.rem(tp, 2)
     sib = tp + 1 - 2 * k
@@ -60,6 +60,19 @@
             i = slot(quad, s)
             cols = pl.ds(nb * COLS if isinstance(nb, int) else pl.multiple_of(nb * COLS, COLS), COLS)
             put(ref.at[pl.ds(s * ROWS, ROWS), cols], ring.at[i], sem.at[i])
+
+    def issue_last():
+        for n in range(2):
+            for s in range(SB):
+                rows = ROWS if s < 3 else FF - 3 * ROWS
+                put(wd.at[pl.ds(s * ROWS, rows), pl.ds((NT - 2 + n) * TILE, TILE)],
+                    ring.at[slot(Q_WD + NB - 1, s), pl.ds(0, rows), pl.ds(n * TILE, TILE)], lsem.at[n, s])
+
+    def last_arrive(n):
+        for s in range(SB):
+            rows = ROWS if s < 3 else FF - 3 * ROWS
+            pltpu.make_async_copy(wd.at[pl.ds(0, rows), pl.ds(0, TILE)],
+                                  ring.at[slot(Q_WD + NB - 1, s), pl.ds(0, rows), pl.ds(n * TILE, TILE)], lsem.at[n, s]).wait()
 
     def issue_wd(nb):
         cols = pl.ds(nb * COLS if isinstance(nb, int) else pl.multiple_of(nb * COLS, COLS), COLS)
@@ -84,8 +97,10 @@
         elif quad < Q_WD:
             n = quad - Q_GU
             issue_gu(wg if n % 2 == 0 else wu, n // 2, quad)
-        elif quad < Q_WD + NB:
+        elif quad < Q_WD + NB - 1:
             issue_wd(quad - Q_WD)
+        elif quad == Q_WD + NB - 1:
+            issue_last()
 
     def arrive(quad, s, rows=ROWS):
         i = slot(quad, s)
@@ -189,85 +204,80 @@
             o = o[0:8, 0:HEAD] + o[8:16, HEAD:TILE]
             seen[pl.ds(g * SB + s, 8, stride=BATCH), :] = o.astype(BF16).astype(F32)
 
-    def rows(e):
-        return pl.ds(0, BATCH if e == 2 else HALF)
-
-    def place(e):
-        return (1, pl.ds(0, BATCH)) if e == 2 else (0, pl.ds(e * HALF, HALF))
-    def remote(src, dst, a, b, peer):
-        return pltpu.make_async_remote_copy(src_ref=src, dst_ref=dst, send_sem=a, recv_sem=b, device_id={"tp": peer},
-                                            device_id_type=pl.DeviceIdType.MESH)
-
-    def copy1(e, c):
-        return remote(s1.at[e, c, 1 - k, rows(e)], r1.at[e, c, rows(e)], ss1.at[e, c], rs1.at[e, c], sib)
-
-    def copy2(e, c):
-        return remote(s2.at[e, c, rows(e)], r2.at[e, c, rows(e)], ss2.at[e, c], rs2.at[e, c], far)
-
-    def copy3(e, c):
-        which, at = place(e)
-        return remote(y.at[which, 2 * c + k, at], y.at[which, 2 * c + k, at], ss3.at[e, c], rs3.at[e, c], sib)
-
-    def stage1(e, c, tiles):
-        for n in range(2):
-            f1[c, n, rows(e)] = tiles[n]
-            s1[e, c, n, rows(e)] = tiles[n].astype(BF16)
-        copy1(e, c).start()
+    def remote(src, dst, stage, n, peer):
+        return pltpu.make_async_remote_copy(src_ref=src, dst_ref=dst, send_sem=xs.at[stage, n], recv_sem=xr.at[stage, n],
+                                            device_id={"tp": peer}, device_id_type=pl.DeviceIdType.MESH)
+
+    class Unit:
+        def __init__(self, e, c):
+            self.e, self.c = e, c
+            if e < 3:
+                t = 2 if e < 2 else 1
+                at = (pl.ds(0, EARLY), pl.ds(EARLY, BATCH - EARLY), pl.ds(0, BATCH))[e]
+                p = e // 2
+                own, other, got = pl.ds(2 * t * c + t * k, t), pl.ds(2 * t * c + t * (1 - k), t), pl.ds(t * c, t)
+                self.n = (0, NB // 2, NB)[e] + c
+                self.term, self.give, self.take = f1.at[own, at], s1.at[p, other, at], r1.at[p, got, at]
+                self.pair, self.far = s2.at[p, got, at], r2.at[p, got, at]
+                self.base = xb.at[own, at] if e < 2 else y.at[0, own]
+                self.result = y.at[p, own, at]
+            else:
+                self.n = 2 * NB + c
+                half = pl.ds(pl.multiple_of(k * 128, 128), 128)
+                self.term, self.give, self.take = fz.at[c, k], sz.at[c, 1 - k], rz.at[c, 0]
+                self.pair, self.far = rz.at[c, 1], rz.at[c, 2]
+                self.base, self.result = y.at[0, NT - 2 + c, :, half], yz.at[c, k]
+
+        def copy1(self):
+            return remote(self.give, self.take, 0, self.n, sib)
+
+        def copy2(self):
+            return remote(self.pair, self.far, 1, self.n, far)
+
+        def copy3(self):
+            return remote(self.result, self.result, 2, self.n, sib)
+
+    def stage1(e, c):
+        Unit(e, c).copy1().start()
 
     def stage2(e, c):
-        copy1(e, c).wait_recv()
-        s2[e, c, rows(e)] = (f1[c, k, rows(e)] + r1[e, c, rows(e)].astype(F32)).astype(BF16)
-        copy2(e, c).start()
+        u = Unit(e, c)
+        u.copy1().wait_recv()
+        u.pair[...] = (u.term[...] + u.take[...].astype(F32)).astype(BF16)
+        u.copy2().start()
 
     def stage3(e, c):
-        copy2(e, c).wait_recv()
-        j = 2 * c + k
-        which, at = place(e)
-        base = (y[0, j] if e == 2 else xb[j, at]).astype(F32)
-        y[which, j, at] = (base + (s2[e, c, rows(e)].astype(F32) + r2[e, c, rows(e)].astype(F32))).astype(BF16)
-        copy3(e, c).start()
+        u = Unit(e, c)
+        u.copy2().wait_recv()
+        u.result[...] = (u.base[...].astype(F32) + (u.pair[...].astype(F32) + u.far[...].astype(F32))).astype(BF16)
+        u.copy3().start()
 
     def stage4(e, c):
-        copy3(e, c).wait_recv()
+        Unit(e, c).copy3().wait_recv()
         if e == 2:
             for j in (2 * c, 2 * c + 1):
                 out[:, j * TILE:(j + 1) * TILE] = y[1, j]
-
-    def behind(e, c):
-        @pl.when(c >= 2)
-        def _():
-            stage2(e, c - 2)
-
-        @pl.when(c >= 5)
-        def _():
-            stage3(e, c - 5)
-
-    def drain(e):
-        for c in range(NB - 2, NB):
-            stage2(e, c)
-        for c in range(NB - 5, NB):
-            stage3(e, c)
-        for c in range(NB):
-            stage4(e, c)
-
-    def sent(e):
-        for c in range(NB):
-            copy1(e, c).wait_send()
-            copy2(e, c).wait_send()
-            copy3(e, c).wait_send()
-
-    def loop(body):
-        def one(c, _):
-            body(c)
-            return 0
-        lax.fori_loop(0, NB, one, 0)
+        elif e == 3:
+            for n in range(2):
+                out[:, (NT - 2 + c) * TILE + n * 128:(NT - 2 + c) * TILE + (n + 1) * 128] = yz[c, n]
+
+    def sent(e, c):
+        u = Unit(e, c)
+        u.copy1().wait_send()
+        u.copy2().wait_send()
+        u.copy3().wait_send()
+
+    def keep(p, j, at, t):
+        f1[j, at] = t
+        s1[p, j, at] = t.astype(BF16)
 
     def wo_steps(e):
-        def one(c):
-            at = e * HALF
-            a = jnp.concatenate([seen[h * BATCH + at:h * BATCH + at + HALF, :].astype(BF16) for h in range(8)], 1)
-            stage1(e, c, [dot(a, held[c, :, n * TILE:(n + 1) * TILE]) for n in range(2)])
-        loop(one)
+        at = slice(0, EARLY) if e == 0 else slice(EARLY, BATCH)
+        a = jnp.concatenate([seen[h * BATCH + at.start:h * BATCH + at.stop, :].astype(BF16) for h in range(8)], 1)
+        for j in range(NT):
+            keep(0, j, at, dot(a, held[j // 2, :, j % 2 * TILE:(j % 2 + 1) * TILE]))
+            if j % 4 == 3:
+                stage1(e, j // 4)
 
     for s in range(SB):
         arrive(Q_K0, s)
@@ -304,20 +314,14 @@
                         issue(Q_KV + 2 * n + R)
                         issue(Q_KV + 1 + 2 * n + R)
 
-        @pl.when(gp == GROUPS // 4 - 1)
+        @pl.when(gp == EARLY // (2 * SB) - 1)
         def _():
             pl.semaphore_wait(barrier, 2)
             for i in range(NB):
                 held_arrive(i)
             wo_steps(0)
-
-        @pl.when(gp == GROUPS // 4)
-        def _():
-            loop(lambda c: stage2(0, c))
-
-        @pl.when(gp == GROUPS // 4 + 1)
-        def _():
-            loop(lambda c: stage3(0, c))
+            for c in range(NB // 2):
+                stage2(0, c)
         return 0
 
     lax.fori_loop(0, GROUPS // 2 - 1, pair, 0)
@@ -330,11 +334,17 @@
     issue(Q_VL + R)
 
     wo_steps(1)
-    loop(lambda c: stage2(1, c))
-    loop(lambda c: stage3(1, c))
-    for e in range(2):
-        for c in range(NB):
-            stage4(e, c)
+    for c in range(NB // 2):
+        stage3(0, c)
+    for c in range(NB // 2):
+        stage2(1, c)
+    for c in range(NB // 2):
+        stage4(0, c)
+        sent(0, c)
+    for c in range(NB // 2):
+        stage3(1, c)
+    for c in range(NB // 2):
+        stage4(1, c)
     normed(lambda j: y[0, j], 1)
 
     def gu_step(nb, _):
@@ -362,31 +372,72 @@
 
     lax.fori_loop(0, NF, gu_step, 0)
 
+    def down(quad, cols):
+        acc = None
+        for kc in range(4):
+            i = slot(quad, kc)
+            if kc < 3:
+                d = dot(jnp.concatenate([hid[2 * kc], hid[2 * kc + 1]], 1), ring[i, :, cols])
+            else:
+                d = dot(hid[NF - 1], ring[i, 0:FF - 3 * ROWS, cols])
+            acc = d if acc is None else acc + d
+        return acc
+
     def wd_step(c, _):
         for s in range(3):
             arrive(Q_WD + c, s)
         arrive(Q_WD + c, 3, FF - 3 * ROWS)
-        tiles = []
         for n in range(2):
-            cols = slice(n * TILE, (n + 1) * TILE)
-            acc = None
-            for kc in range(4):
-                i = slot(Q_WD + c, kc)
-                if kc < 3:
-                    d = dot(jnp.concatenate([hid[2 * kc], hid[2 * kc + 1]], 1), ring[i, :, cols])
-                else:
-                    d = dot(hid[NF - 1], ring[i, 0:FF - 3 * ROWS, cols])
-                acc = d if acc is None else acc + d
-            tiles.append(acc)
-        stage1(2, c, tiles)
-        behind(2, c)
+            keep(1, 2 * c + n, slice(0, BATCH), down(Q_WD + c, slice(n * TILE, (n + 1) * TILE)))
+        stage1(2, c)
+
+        @pl.when(c >= 2)
+        def _():
+            stage2(2, c - 2)
+
+        @pl.when(c >= 5)
+        def _():
+            stage3(2, c - 5)
         return 0
 
-    sent(0)
-    sent(1)
-    lax.fori_loop(0, NB, wd_step, 0)
-    drain(2)
-    sent(2)
+    for c in range(NB // 2):
+        sent(1, c)
+    lax.fori_loop(0, NB - 1, wd_step, 0)
+
+    def finish(n):
+        last_arrive(n)
+        t = down(Q_WD + NB - 1, slice(n * TILE, (n + 1) * TILE))
+        for h in range(2):
+            fz[n, h] = t[:, h * 128:(h + 1) * 128]
+            sz[n, h] = t[:, h * 128:(h + 1) * 128].astype(BF16)
+        stage1(3, n)
+
+    finish(0)
+    stage2(2, NB - 3)
+    finish(1)
+    stage2(2, NB - 2)
+    stage2(3, 0)
+    stage3(2, NB - 6)
+    stage3(2, NB - 5)
+    stage2(3, 1)
+    stage3(2, NB - 4)
+    stage3(2, NB - 3)
+    for c in range(NB - 4):
+        stage4(2, c)
+        sent(2, c)
+    stage3(2, NB - 2)
+    stage3(3, 0)
+    stage4(2, NB - 4)
+    stage4(2, NB - 3)
+    stage3(3, 1)
+    for c in range(NB - 4, NB - 1):
+        if c == NB - 2:
+            stage4(2, c)
+        sent(2, c)
+    for n in range(2):
+        stage4(3, n)
+    for n in range(2):
+        sent(3, n)
 
 
 def solution(mesh):
@@ -417,14 +468,18 @@
                 pltpu.VMEM((SB, 2, 16, ROWS), F32),
                 pltpu.VMEM((8 * BATCH, HEAD), F32),
                 pltpu.VMEM((NF, BATCH, COLS), BF16),
-                pltpu.VMEM((NB, 2, BATCH, TILE), F32),
-                pltpu.VMEM((3, NB, 2, BATCH, TILE), BF16),
-                pltpu.VMEM((3, NB, BATCH, TILE), BF16),
-                pltpu.VMEM((3, NB, BATCH, TILE), BF16),
-                pltpu.VMEM((3, NB, BATCH, TILE), BF16),
+                pltpu.VMEM((NT, BATCH, TILE), F32),
                 pltpu.VMEM((2, NT, BATCH, TILE), BF16),
-                dma((R * SB,)), dma((NB,)), dma((NT,)), dma((3,)),
-                *[dma((3, NB))] * 6,
+                pltpu.VMEM((2, NB, BATCH, TILE), BF16),
+                pltpu.VMEM((2, NB, BATCH, TILE), BF16),
+                pltpu.VMEM((2, NB, BATCH, TILE), BF16),
+                pltpu.VMEM((2, NT, BATCH, TILE), BF16),
+                pltpu.VMEM((2, 2, BATCH, 128), F32),
+                pltpu.VMEM((2, 2, BATCH, 128), BF16),
+                pltpu.VMEM((2, 3, BATCH, 128), BF16),
+                pltpu.VMEM((2, 2, BATCH, 128), BF16),
+                dma((R * SB,)), dma((NB,)), dma((2, SB)), dma((NT,)), dma((3,)),
+                dma((3, 2 * NB + 2)), dma((3, 2 * NB + 2)),
             ],
             compiler_params=pltpu.CompilerParams(collective_id=0, has_side_effects=True, vmem_limit_bytes=65_900_000),
             cost_estimate=pl.CostEstimate(flops=20 * 10**9, bytes_accessed=240 * 10**6, transcendentals=0),

time: 82.1 us -> 81.3 us (level)
    pallas_call x1, Pallas kernels: 81.2 us -> 80.4 us  [step(): call(x, k_cache.reshape(flat), v_cache.reshape(flat), gain_a.reshape(D //...]
where the time goes in v3:
time: 81.3 us; the launch traced here: 81.2 us
  Pallas kernels  80.4 us (99%)
    pallas_call x1, Pallas kernels, step(): call(x, k_cache.reshape(flat), v_cache.reshape(flat), gain_a.reshape(D //...  80.4 us

profile of v3, /device:TPU:0, one launch (start us, length us, event | category | flops | bytes accessed | tf_op | source)
XLA Modules:
  0.0 81.2 jit_solution(8660022146818190170)
XLA Ops:
  0.0 80.4 %layer.1 = bf16[64,4096]{1,0:T(8,128)(2,1)S(1)} custom-call(bf16[64,4096]{1,0:T(8,128)(2,1)} %x_hbm.1, bf16[64,4096,128]{2,1,0:T(8,128)(2,1)} %bitcast.k_hbm, bf16[64,4096,128]{2,1,0:T(8,128)(2,1)} %bitcast.1.v_hbm, bf16[32,128]{1,0:T(8,128)(2,1)} %bitcast.4, bf16[4096,1024]{1,0:T(8,128)(2,1)} %wq.1, bf16[1024,4096]{1,0:T(8,128)(2,1)} %wo.1, ...), custom_call_target="tpu_custom_call" | custom-call | flops 20000000000 | bytes 240000000 | tf_op jit(solution)/shard_map/layer/pallas_call | solution.py:488
  80.4 0.8 copy.13

commit v4 on v3

--- a/solution.py
+++ b/solution.py
@@ -29,59 +29,64 @@
 
 def kernel(x_hbm, k_hbm, v_hbm, ga_hbm, wq, wo, gm_hbm, wg, wu, wd, rot_hbm, out,
            ring, held, xb, ab, gb, rb, qb, sca, scb, seen, hid, f1, s1, r1, s2, r2, y,
-           fz, sz, rz, yz, sem, wsem, lsem, xsem, gsem, xs, xr):
+           fz, sz, rz, yz, sem, dsem, wsem, lsem, xsem, gsem, xs, xr):
     tp = lax.axis_index("tp")
     k = lax.rem(tp, 2)
     sib = tp + 1 - 2 * k
     far = lax.rem(tp + 2, 4)
 
+    def spot(quad):
+        return quad % R if isinstance(quad, int) else lax.rem(quad, R)
+
     def slot(quad, s):
-        return (quad % R if isinstance(quad, int) else lax.rem(quad, R)) * SB + s
+        return spot(quad) * SB + s
+
+    def filled(ref, sem):
+        pltpu.make_async_copy(ref, ref, sem).wait()
 
     def put(src, dst, s):
         pltpu.make_async_copy(src, dst, s).start(priority=1)
 
     def issue_wq():
         for i in range(2 * SB):
-            pltpu.make_async_copy(wq.at[pl.ds(i % SB * ROWS, ROWS), pl.ds(i // SB * COLS, COLS)], held.at[i], wsem.at[i]).start()
+            pltpu.make_async_copy(wq.at[pl.ds(i % SB * ROWS, ROWS), pl.ds(i // SB * COLS, COLS)], held.at[i], wsem.at[i // SB]).start()
 
     def issue_kv(ref, g, quad):
         for s in range(SB):
             i = slot(quad, s)
             for c in range(4):
-                put(ref.at[g * SB + s, pl.ds(c * ROWS, ROWS), :], ring.at[i, :, pl.ds(c * 128, 128)], sem.at[i])
+                put(ref.at[g * SB + s, pl.ds(c * ROWS, ROWS), :], ring.at[i, :, pl.ds(c * 128, 128)], sem.at[spot(quad)])
 
     def issue_wo():
         for i in range(NB):
-            put(wo.at[:, pl.ds(i * COLS, COLS)], held.at[i], wsem.at[i])
+            put(wo.at[:, pl.ds(i * COLS, COLS)], held.at[i], wsem.at[i // SB])
 
     def issue_gu(ref, nb, quad):
         for s in range(SB):
             i = slot(quad, s)
             cols = pl.ds(nb * COLS if isinstance(nb, int) else pl.multiple_of(nb * COLS, COLS), COLS)
-            put(ref.at[pl.ds(s * ROWS, ROWS), cols], ring.at[i], sem.at[i])
+            put(ref.at[pl.ds(s * ROWS, ROWS), cols], ring.at[i], sem.at[spot(quad)])
 
     def issue_last():
         for n in range(2):
             for s in range(SB):
                 rows = ROWS if s < 3 else FF - 3 * ROWS
                 put(wd.at[pl.ds(s * ROWS, rows), pl.ds((NT - 2 + n) * TILE, TILE)],
-                    ring.at[slot(Q_WD + NB - 1, s), pl.ds(0, rows), pl.ds(n * TILE, TILE)], lsem.at[n, s])
+                    ring.at[slot(Q_WD + NB - 1, s), pl.ds(0, rows), pl.ds(n * TILE, TILE)], lsem.at[n, s // 3])
 
     def last_arrive(n):
-        for s in range(SB):
-            rows = ROWS if s < 3 else FF - 3 * ROWS
-            pltpu.make_async_copy(wd.at[pl.ds(0, rows), pl.ds(0, TILE)],
-                                  ring.at[slot(Q_WD + NB - 1, s), pl.ds(0, rows), pl.ds(n * TILE, TILE)], lsem.at[n, s]).wait()
+        cols = pl.ds(n * TILE, TILE)
+        filled(ring.at[pl.ds(slot(Q_WD + NB - 1, 0), 3), :, cols], lsem.at[n, 0])
+        filled(ring.at[slot(Q_WD + NB - 1, 3), pl.ds(0, FF - 3 * ROWS), cols], lsem.at[n, 1])
 
     def issue_wd(nb):
         cols = pl.ds(nb * COLS if isinstance(nb, int) else pl.multiple_of(nb * COLS, COLS), COLS)
         for s in range(SB):
             i = slot(Q_WD + nb, s)
             if s < 3:
-                put(wd.at[pl.ds(s * ROWS, ROWS), cols], ring.at[i], sem.at[i])
+                put(wd.at[pl.ds(s * ROWS, ROWS), cols], ring.at[i], sem.at[spot(Q_WD + nb)])
             else:
-                put(wd.at[pl.ds(s * ROWS, FF - 3 * ROWS), cols], ring.at[i, pl.ds(0, FF - 3 * ROWS), :], sem.at[i])
+                put(wd.at[pl.ds(s * ROWS, FF - 3 * ROWS), cols], ring.at[i, pl.ds(0, FF - 3 * ROWS), :], dsem.at[nb])
 
     def issue(quad):
         if quad == Q_K0:
@@ -102,14 +107,13 @@
         elif quad == Q_WD + NB - 1:
             issue_last()
 
-    def arrive(quad, s, rows=ROWS):
-        i = slot(quad, s)
-        pltpu.make_async_copy(wq.at[pl.ds(0, rows), pl.ds(0, COLS)], ring.at[i, pl.ds(0, rows), :], sem.at[i]).wait()
-
-    def held_arrive(i):
-        pltpu.make_async_copy(wq.at[pl.ds(0, ROWS), pl.ds(0, COLS)], held.at[i], wsem.at[i]).wait()
-
-    xcopies = [pltpu.make_async_copy(x_hbm.at[:, pl.ds(j * TILE, TILE)], xb.at[j], xsem.at[j]) for j in range(NT)]
+    def arrive(quad, slots=SB):
+        filled(ring.at[pl.ds(slot(quad, 0), slots)], sem.at[spot(quad)])
+
+    def held_arrive(part):
+        filled(held.at[pl.ds(part * SB, SB)], wsem.at[part])
+
+    xcopies = [pltpu.make_async_copy(x_hbm.at[:, pl.ds(j * TILE, TILE)], xb.at[j], xsem) for j in range(NT)]
     small = [pltpu.make_async_copy(a, b, gsem.at[n]) for n, (a, b) in enumerate(
         ((ga_hbm, gb.at[0]), (gm_hbm, gb.at[1]), (rot_hbm, rb)))]
     for c in xcopies + small:
@@ -122,7 +126,8 @@
     for peer in (sib, far):
         pl.semaphore_signal(barrier, inc=1, device_id={"tp": peer}, device_id_type=pl.DeviceIdType.MESH)
 
-    for c in xcopies + small:
+    filled(xb, xsem)
+    for c in small:
         c.wait()
 
     def normed(src, gain):
@@ -148,8 +153,7 @@
 
     cos, sin = rb[0:1, :], rb[1:2, :]
     for nc in range(2):
-        for s in range(SB):
-            held_arrive(nc * SB + s)
+        held_arrive(nc)
         for n in range(2):
             acc = None
             for kc in range(4):
@@ -205,24 +209,24 @@
             seen[pl.ds(g * SB + s, 8, stride=BATCH), :] = o.astype(BF16).astype(F32)
 
     def remote(src, dst, stage, n, peer):
-        return pltpu.make_async_remote_copy(src_ref=src, dst_ref=dst, send_sem=xs.at[stage, n], recv_sem=xr.at[stage, n],
+        return pltpu.make_async_remote_copy(src_ref=src, dst_ref=dst, send_sem=xs.at[n], recv_sem=xr.at[stage, n],
                                             device_id={"tp": peer}, device_id_type=pl.DeviceIdType.MESH)
 
     class Unit:
         def __init__(self, e, c):
             self.e, self.c = e, c
             if e < 3:
-                t = 2 if e < 2 else 1
+                t = 4 if e < 2 else 1
                 at = (pl.ds(0, EARLY), pl.ds(EARLY, BATCH - EARLY), pl.ds(0, BATCH))[e]
                 p = e // 2
                 own, other, got = pl.ds(2 * t * c + t * k, t), pl.ds(2 * t * c + t * (1 - k), t), pl.ds(t * c, t)
-                self.n = (0, NB // 2, NB)[e] + c
+                self.n = (0, 2, 4)[e] + c
                 self.term, self.give, self.take = f1.at[own, at], s1.at[p, other, at], r1.at[p, got, at]
                 self.pair, self.far = s2.at[p, got, at], r2.at[p, got, at]
                 self.base = xb.at[own, at] if e < 2 else y.at[0, own]
                 self.result = y.at[p, own, at]
             else:
-                self.n = 2 * NB + c
+                self.n = NB + 3 + c
                 half = pl.ds(pl.multiple_of(k * 128, 128), 128)
                 self.term, self.give, self.take = fz.at[c, k], sz.at[c, 1 - k], rz.at[c, 0]
                 self.pair, self.far = rz.at[c, 1], rz.at[c, 2]
@@ -244,12 +248,14 @@
         u = Unit(e, c)
         u.copy1().wait_recv()
         u.pair[...] = (u.term[...] + u.take[...].astype(F32)).astype(BF16)
+        u.copy1().wait_send()
         u.copy2().start()
 
     def stage3(e, c):
         u = Unit(e, c)
         u.copy2().wait_recv()
         u.result[...] = (u.base[...].astype(F32) + (u.pair[...].astype(F32) + u.far[...].astype(F32))).astype(BF16)
+        u.copy2().wait_send()
         u.copy3().start()
 
     def stage4(e, c):
@@ -262,10 +268,7 @@
                 out[:, (NT - 2 + c) * TILE + n * 128:(NT - 2 + c) * TILE + (n + 1) * 128] = yz[c, n]
 
     def sent(e, c):
-        u = Unit(e, c)
-        u.copy1().wait_send()
-        u.copy2().wait_send()
-        u.copy3().wait_send()
+        Unit(e, c).copy3().wait_send()
 
     def keep(p, j, at, t):
         f1[j, at] = t
@@ -276,19 +279,17 @@
         a = jnp.concatenate([seen[h * BATCH + at.start:h * BATCH + at.stop, :].astype(BF16) for h in range(8)], 1)
         for j in range(NT):
             keep(0, j, at, dot(a, held[j // 2, :, j % 2 * TILE:(j % 2 + 1) * TILE]))
-            if j % 4 == 3:
-                stage1(e, j // 4)
-
-    for s in range(SB):
-        arrive(Q_K0, s)
+            if j % 8 == 7:
+                stage1(e, j // 8)
+
+    arrive(Q_K0)
     scores(0, Q_K0, sca)
     issue(R + Q_K0)
 
     def half(g, read, write):
         kq, vq = Q_KV + 2 * g, Q_KV + 1 + 2 * g
-        for s in range(SB):
-            arrive(kq, s)
-            arrive(vq, s)
+        arrive(kq)
+        arrive(vq)
         scores(g + 1, kq, write)
         attend(g, vq, read)
 
@@ -317,10 +318,10 @@
         @pl.when(gp == EARLY // (2 * SB) - 1)
         def _():
             pl.semaphore_wait(barrier, 2)
-            for i in range(NB):
-                held_arrive(i)
+            held_arrive(0)
+            held_arrive(1)
             wo_steps(0)
-            for c in range(NB // 2):
+            for c in range(2):
                 stage2(0, c)
         return 0
 
@@ -328,30 +329,28 @@
     half(GROUPS - 2, sca, scb)
     issue(Q_KV + 2 * (GROUPS - 2) + R)
     issue(Q_KV + 1 + 2 * (GROUPS - 2) + R)
-    for s in range(SB):
-        arrive(Q_VL, s)
+    arrive(Q_VL)
     attend(GROUPS - 1, Q_VL, scb)
     issue(Q_VL + R)
 
     wo_steps(1)
-    for c in range(NB // 2):
+    for c in range(2):
         stage3(0, c)
-    for c in range(NB // 2):
+    for c in range(2):
         stage2(1, c)
-    for c in range(NB // 2):
+    for c in range(2):
         stage4(0, c)
         sent(0, c)
-    for c in range(NB // 2):
+    for c in range(2):
         stage3(1, c)
-    for c in range(NB // 2):
+    for c in range(2):
         stage4(1, c)
     normed(lambda j: y[0, j], 1)
 
     def gu_step(nb, _):
         gq, uq = Q_GU + 2 * nb, Q_GU + 1 + 2 * nb
-        for s in range(SB):
-            arrive(gq, s)
-            arrive(uq, s)
+        arrive(gq)
+        arrive(uq)
         for n in range(2):
             cols = slice(n * TILE, (n + 1) * TILE)
             gate = up = None
@@ -373,69 +372,62 @@
     lax.fori_loop(0, NF, gu_step, 0)
 
     def down(quad, cols):
-        acc = None
+        parts = []
         for kc in range(4):
             i = slot(quad, kc)
             if kc < 3:
-                d = dot(jnp.concatenate([hid[2 * kc], hid[2 * kc + 1]], 1), ring[i, :, cols])
+                parts.append(dot(jnp.concatenate([hid[2 * kc], hid[2 * kc + 1]], 1), ring[i, :, cols]))
             else:
-                d = dot(hid[NF - 1], ring[i, 0:FF - 3 * ROWS, cols])
-            acc = d if acc is None else acc + d
-        return acc
+                parts.append(dot(hid[NF - 1], ring[i, 0:FF - 3 * ROWS, cols]))
+        return parts[0] + parts[1], parts[2] + parts[3]
 
     def wd_step(c, _):
-        for s in range(3):
-            arrive(Q_WD + c, s)
-        arrive(Q_WD + c, 3, FF - 3 * ROWS)
+        arrive(Q_WD + c, 3)
+        filled(ring.at[slot(Q_WD + c, 3), pl.ds(0, FF - 3 * ROWS)], dsem.at[c])
         for n in range(2):
-            keep(1, 2 * c + n, slice(0, BATCH), down(Q_WD + c, slice(n * TILE, (n + 1) * TILE)))
+            keep(1, 2 * c + n, slice(0, BATCH), sum(down(Q_WD + c, slice(n * TILE, (n + 1) * TILE))))
         stage1(2, c)
 
-        @pl.when(c >= 2)
+        @pl.when(c >= 1)
         def _():
-            stage2(2, c - 2)
-
-        @pl.when(c >= 5)
-        def _():
-            stage3(2, c - 5)
+            stage2(2, c - 1)
         return 0
 
-    for c in range(NB // 2):
+    for c in range(2):
         sent(1, c)
     lax.fori_loop(0, NB - 1, wd_step, 0)
 
     def finish(n):
-        last_arrive(n)
-        t = down(Q_WD + NB - 1, slice(n * TILE, (n + 1) * TILE))
+        a, b = down(Q_WD + NB - 1, slice(n * TILE, (n + 1) * TILE))
+        t = a + jnp.where(k >= 0, b, 0.0)
         for h in range(2):
             fz[n, h] = t[:, h * 128:(h + 1) * 128]
             sz[n, h] = t[:, h * 128:(h + 1) * 128].astype(BF16)
         stage1(3, n)
 
+    last_arrive(0)
     finish(0)
-    stage2(2, NB - 3)
+    last_arrive(1)
     finish(1)
     stage2(2, NB - 2)
     stage2(3, 0)
-    stage3(2, NB - 6)
-    stage3(2, NB - 5)
+    for c in range(NB - 4):
+        stage3(2, c)
     stage2(3, 1)
     stage3(2, NB - 4)
     stage3(2, NB - 3)
     for c in range(NB - 4):
         stage4(2, c)
-        sent(2, c)
     stage3(2, NB - 2)
     stage3(3, 0)
     stage4(2, NB - 4)
     stage4(2, NB - 3)
     stage3(3, 1)
-    for c in range(NB - 4, NB - 1):
-        if c == NB - 2:
-            stage4(2, c)
-        sent(2, c)
+    stage4(2, NB - 2)
     for n in range(2):
         stage4(3, n)
+    for c in range(NB - 1):
+        sent(2, c)
     for n in range(2):
         sent(3, n)
 
@@ -478,8 +470,8 @@
                 pltpu.VMEM((2, 2, BATCH, 128), BF16),
                 pltpu.VMEM((2, 3, BATCH, 128), BF16),
                 pltpu.VMEM((2, 2, BATCH, 128), BF16),
-                dma((R * SB,)), dma((NB,)), dma((2, SB)), dma((NT,)), dma((3,)),
-                dma((3, 2 * NB + 2)), dma((3, 2 * NB + 2)),
+                dma((R,)), dma((NB - 1,)), dma((2,)), dma((2, 2)), dma(()), dma((3,)),
+                dma((NB + 5,)), dma((3, NB + 5)),
             ],
             compiler_params=pltpu.CompilerParams(collective_id=0, has_side_effects=True, vmem_limit_bytes=65_900_000),
             cost_estimate=pl.CostEstimate(flops=20 * 10**9, bytes_accessed=240 * 10**6, transcendentals=0),

time: 81.3 us -> 79.1 us (0.973)
  Pallas kernels: 80.4 us -> 78.2 us
    pallas_call x1, Pallas kernels: 80.4 us -> 78.2 us  [step(): call(x, k_cache.reshape(flat), v_cache.reshape(flat), gain_a.reshape(D //...]
where the time goes in v4:
time: 79.1 us; the launch traced here: 79 us
  Pallas kernels  78.2 us (99%)
  local copies, waits for them, and re-layouts  0.8 us (1%)
    pallas_call x1, Pallas kernels, step(): call(x, k_cache.reshape(flat), v_cache.reshape(flat), gain_a.reshape(D //...  78.2 us

profile of v4, /device:TPU:0, one launch (start us, length us, event | category | flops | bytes accessed | tf_op | source)
XLA Modules:
  0.0 79.0 jit_solution(12254072651509476088)
XLA Ops:
  0.0 78.2 %layer.1 = bf16[64,4096]{1,0:T(8,128)(2,1)S(1)} custom-call(bf16[64,4096]{1,0:T(8,128)(2,1)} %x_hbm.1, bf16[64,4096,128]{2,1,0:T(8,128)(2,1)} %bitcast.k_hbm, bf16[64,4096,128]{2,1,0:T(8,128)(2,1)} %bitcast.1.v_hbm, bf16[32,128]{1,0:T(8,128)(2,1)} %bitcast.4, bf16[4096,1024]{1,0:T(8,128)(2,1)} %wq.1, bf16[1024,4096]{1,0:T(8,128)(2,1)} %wo.1, ...), custom_call_target="tpu_custom_call" | custom-call | flops 20000000000 | bytes 240000000 | tf_op jit(solution)/shard_map/layer/pallas_call | solution.py:480
  78.2 0.8 %copy.13 = bf16[64,4096]{1,0:T(8,128)(2,1)} copy(bf16[64,4096]{1,0:T(8,128)(2,1)S(1)} %layer.1) | data formatting | bytes 1048576

commit v5 on v4

--- a/solution.py
+++ b/solution.py
@@ -409,10 +409,10 @@
     finish(0)
     last_arrive(1)
     finish(1)
+    for c in range(NB - 4):
+        stage3(2, c)
     stage2(2, NB - 2)
     stage2(3, 0)
-    for c in range(NB - 4):
-        stage3(2, c)
     stage2(3, 1)
     stage3(2, NB - 4)
     stage3(2, NB - 3)

time: 79.1 us -> 79.5 us (level)
  no operation moved by 1% of the time
where the time goes in v5:
time: 79.5 us; the launch traced here: 79.4 us
  Pallas kernels  78.6 us (99%)
  local copies, waits for them, and re-layouts  0.8 us (1%)
    pallas_call x1, Pallas kernels, step(): call(x, k_cache.reshape(flat), v_cache.reshape(flat), gain_a.reshape(D //...  78.6 us

profile of v5, /device:TPU:0, one launch (start us, length us, event | category | flops | bytes accessed | tf_op | source)
XLA Modules:
  0.0 79.4 jit_solution(15288420110491963726)
XLA Ops:
  0.0 78.6 %layer.1 = bf16[64,4096]{1,0:T(8,128)(2,1)S(1)} custom-call(bf16[64,4096]{1,0:T(8,128)(2,1)} %x_hbm.1, bf16[64,4096,128]{2,1,0:T(8,128)(2,1)} %bitcast.k_hbm, bf16[64,4096,128]{2,1,0:T(8,128)(2,1)} %bitcast.1.v_hbm, bf16[32,128]{1,0:T(8,128)(2,1)} %bitcast.4, bf16[4096,1024]{1,0:T(8,128)(2,1)} %wq.1, bf16[1024,4096]{1,0:T(8,128)(2,1)} %wo.1, ...), custom_call_target="tpu_custom_call" | custom-call | flops 20000000000 | bytes 240000000 | tf_op jit(solution)/shard_map/layer/pallas_call | solution.py:480
  78.6 0.8 %copy.13 = bf16[64,4096]{1,0:T(8,128)(2,1)} copy(bf16[64,4096]{1,0:T(8,128)(2,1)S(1)} %layer.1) | data formatting | bytes 1048576
